TPU v7x, 32 devices: a whole 2x2x4 slice. The times are simulated.
32 devices in a mesh: expert: 8 (over z, y), tensor: 4 (over x, core).
Axes of the slice: x: 2, y: 2, z: 4, core: 2. Of those that a mesh axis runs over, the one named last changes fastest.
Arguments:
- tokens: bfloat16 [1024, 2880], P(('expert', 'tensor')), may hold values from -6 to 6
- cotangent: bfloat16 [1024, 2880], P(('expert', 'tensor')), may hold values from -6 to 6
- routes: int32 [1024, 4], P(('expert', 'tensor')), may hold values from 0 to 7, all different within a row; in each aligned block of 32 rows (0 to 31, 32 to 63, ...) at most 24 rows name the same one
- combine: float32 [1024, 4], P(('expert', 'tensor')), may hold values from 0.1 to 1
- w_gate: bfloat16 [8, 2880, 1440], P('expert', None, 'tensor'), may hold values from -0.109375 to 0.109375
- w_up: bfloat16 [8, 2880, 1440], P('expert', None, 'tensor'), may hold values from -0.109375 to 0.109375
- w_down: bfloat16 [8, 1440, 2880], P('expert', 'tensor'), may hold values from -0.15625 to 0.15625
Outputs:
- token_grad: bfloat16 [1024, 2880], P(('expert', 'tensor'))
- gate_grad: bfloat16 [8, 2880, 1440], P('expert', None, 'tensor')
- up_grad: bfloat16 [8, 2880, 1440], P('expert', None, 'tensor')
- down_grad: bfloat16 [8, 1440, 2880], P('expert', 'tensor')
Inputs may be any that keep to these rules, and one draw needn't show every extreme that they name: `routes`: each row names 4 different experts. Among the rows of one device no expert is named more than 24 times, and in every draw some expert is named exactly 24 times by the rows of some device.
All inputs are finite; a program needn't handle non-finite values.
Results may differ from a plain program's by a relative error of at most 0.0065.
Values may be sent and summed in bfloat16 or wider, within the bound.
A program may use at most 128 MiB of HBM per device.

v0:
```python
import jax
import jax.numpy as jnp
from jax import lax
from jax.sharding import PartitionSpec as P


def route_slots(flat, experts, cap):
    onehot = (flat[:, None] == jnp.arange(experts, dtype=jnp.int32)[None, :]).astype(jnp.int32)
    before = jnp.cumsum(onehot, axis=0) - onehot
    place = jnp.sum(before * onehot, axis=1)
    return flat * cap + place


def contract_rows(left, right):
    return lax.dot_general(
        left, right, (((0,), (0,)), ((), ())), preferred_element_type=jnp.float32
    )


def contract_cols(left, right):
    return lax.dot_general(
        left, right, (((1,), (1,)), ((), ())), preferred_element_type=jnp.float32
    )


def on_device(tokens, cotangent, routes, combine, w_gate, w_up, w_down):
    tok_rows, width = tokens.shape
    top_count = routes.shape[1]
    groups = lax.axis_size("expert")
    experts = groups * w_gate.shape[0]
    cap = max(2, 3 * tok_rows * top_count // (2 * experts))
    flat = routes.reshape(-1)
    slot = route_slots(flat, experts, cap)
    target = jnp.arange(experts * cap, dtype=jnp.int32)
    match = slot[None, :] == target[:, None]
    valid = jnp.any(match, axis=1)
    order = jnp.arange(flat.shape[0], dtype=jnp.int32)
    source = jnp.sum(jnp.where(match, order[None, :], 0), axis=1)
    token = source // top_count
    send_x = jnp.where(valid[:, None], tokens[token], jnp.zeros((), tokens.dtype))
    scaled = combine.reshape(-1)[source][:, None] * cotangent[token].astype(jnp.float32)
    send_dy = jnp.where(valid[:, None], scaled, 0.0).astype(jnp.bfloat16)
    send_x = send_x.reshape(groups, cap, width)
    send_dy = send_dy.reshape(groups, cap, width)
    recv_x, recv_dy = (
        lax.all_to_all(send_x, "expert", split_axis=0, concat_axis=0, tiled=True),
        lax.all_to_all(send_dy, "expert", split_axis=0, concat_axis=0, tiled=True),
    )
    recv_x = recv_x.reshape(groups * cap, width)
    recv_dy = recv_dy.reshape(groups * cap, width)
    xs, dys = (
        lax.all_gather(recv_x, "tensor", axis=0, tiled=True),
        lax.all_gather(recv_dy, "tensor", axis=0, tiled=True),
    )
    gate_w = w_gate[0]
    up_w = w_up[0]
    down_w = w_down[0]
    gate = jnp.dot(xs, gate_w, preferred_element_type=jnp.float32)
    upper = jnp.dot(xs, up_w, preferred_element_type=jnp.float32)
    sigma = jax.nn.sigmoid(gate)
    act = (gate * sigma * upper).astype(jnp.bfloat16)
    d_act = contract_cols(dys, down_w)
    down_grad = contract_rows(act, dys).astype(jnp.bfloat16)
    d_upper = (d_act * gate * sigma).astype(jnp.bfloat16)
    d_gate = (d_act * upper * sigma * (1.0 + gate * (1.0 - sigma))).astype(jnp.bfloat16)
    gate_grad = contract_rows(xs, d_gate).astype(jnp.bfloat16)
    up_grad = contract_rows(xs, d_upper).astype(jnp.bfloat16)
    own = lax.psum_scatter(
        contract_cols(d_gate, gate_w) + contract_cols(d_upper, up_w),
        "tensor",
        scatter_dimension=0,
        tiled=True,
    )
    own = own.astype(jnp.bfloat16).reshape(groups, cap, width)
    back = lax.all_to_all(own, "expert", split_axis=0, concat_axis=0, tiled=True).reshape(
        experts * cap, width
    )
    picked = back[slot].astype(jnp.float32).reshape(tok_rows, top_count, width)
    token_grad = jnp.sum(picked, axis=1).astype(jnp.bfloat16)
    return (token_grad, gate_grad[None], up_grad[None], down_grad[None])


def solution(mesh):
    in_specs = (
        P(("expert", "tensor"), None),
        P(("expert", "tensor"), None),
        P(("expert", "tensor"), None),
        P(("expert", "tensor"), None),
        P("expert", None, "tensor"),
        P("expert", None, "tensor"),
        P("expert", "tensor", None),
    )
    out_specs = (
        P(("expert", "tensor"), None),
        P("expert", None, "tensor"),
        P("expert", None, "tensor"),
        P("expert", "tensor", None),
    )
    return jax.shard_map(
        on_device, mesh=mesh, in_specs=in_specs, out_specs=out_specs, check_vma=False
    )
```

profile of v0, /device:TPU:0, one launch (start us, length us, event | category | flops | bytes accessed | tf_op | source)
XLA Modules:
  0.0 255.3 jit_solution(1129990801730708629)
XLA Ops:
  7.2 0.9 copy.17
  9.1 1.3 gather_fusion.2
  10.7 35.4 %all_to_all.15 = bf16[8,24,2880]{2,1,0:T(8,128)(2,1)} all-to-all(bf16[8,24,2880]{2,1,0:T(8,128)(2,1)S(1)} %broadcast_select_fusion), channel_id=1, replica_groups=mesh['expert'=8,'tensor'=4] {'expert'}, dimensions={0} | all-to-all | bytes 2211840 | tf_op jit(solution)/shard_map/all_to_all | solution.py:46
  46.4 1.6 gather_fusion
  48.0 1.4 gather_fusion.1
  49.4 0.4 fusion.4
  49.8 30.9 %all_to_all.16 = bf16[8,24,2880]{2,1,0:T(8,128)(2,1)} all-to-all(bf16[8,24,2880]{2,1,0:T(8,128)(2,1)S(1)} %fusion.4), channel_id=1, replica_groups=mesh['expert'=8,'tensor'=4] {'expert'}, dimensions={0} | all-to-all | bytes 2211840 | tf_op jit(solution)/shard_map/all_to_all | solution.py:47
  80.8 0.3 all-gather.5.cloned.1.call-done
  81.1 4.3 %fusion.7 = f32[768,360]{0,1:T(8,128)S(1)} fusion(bf16[768,2880]{1,0:T(8,128)(2,1)} %all-gather.5.cloned.1.call-done, bf16[1,2880,360]{1,2,0:T(8,128)(2,1)S(1)} %copy-done), kind=kOutput, calls=%fused_computation.16 | convolution fusion | flops 1592524800 | bytes 7603200 | tf_op jit(solution)/shard_map/dot_general | solution.py:58
  85.4 2.9 %fusion.10 = f32[768,360]{0,1:T(8,128)} fusion(bf16[768,2880]{1,0:T(8,128)(2,1)S(1)} %copy-done.10, bf16[1,2880,360]{1,2,0:T(8,128)(2,1)S(1)} %copy-done.3), kind=kOutput, calls=%fused_computation.19 | convolution fusion | flops 1592524800 | bytes 7603200 | tf_op jit(solution)/shard_map/dot_general | solution.py:59
  88.4 30.6 %all-gather.3.cloned.1.call-done = bf16[768,2880]{1,0:T(8,128)(2,1)} async-done(((bf16[192,2880]{1,0:T(8,128)(2,1)}), bf16[768,2880]{1,0:T(8,128)(2,1)}) %all-gather.3.cloned.1.call-update) | async-done | bytes 4423696 | tf_op jit(solution)/shard_map/all_gather | solution.py:53
  119.0 5.3 %multiply_convert_fusion.1 = (bf16[768,360]{0,1:T(8,128)(2,1)S(1)}, bf16[768,360]{0,1:T(8,128)(2,1)S(1)}) fusion(f32[768,360]{0,1:T(8,128)S(1)} %fusion.7, f32[768,360]{0,1:T(8,128)} %fusion.10, bf16[768,2880]{1,0:T(8,128)(2,1)} %all-gather.3.cloned.1.call-done, bf16[1,360,2880]{2,1,0:T(8,128)(2,1)} %param.13), kind=kOutput, calls=%fused_computation.25 | convolution fusion | flops 1596119040 | bytes 9815040 | tf_op jit(solution)/shard_map/dot_general | solution.py:21
  124.3 2.7 %fusion.5 = f32[768,2880]{1,0:T(8,128)S(1)} fusion(bf16[768,360]{0,1:T(8,128)(2,1)S(1)} %get-tuple-element.5, bf16[1,2880,360]{1,2,0:T(8,128)(2,1)S(1)} %copy-done), kind=kOutput, calls=%fused_computation.14 | convolution fusion | flops 1592524800 | bytes 11473920 | tf_op jit(solution)/shard_map/dot_general | solution.py:21
  127.0 5.2 %convolution_add_fusion = f32[768,2880]{1,0:T(8,128)} fusion(f32[768,2880]{1,0:T(8,128)S(1)} %fusion.5, bf16[768,360]{0,1:T(8,128)(2,1)S(1)} %get-tuple-element.4, bf16[1,2880,360]{1,2,0:T(8,128)(2,1)S(1)} %copy-done.4), kind=kOutput, calls=%fused_computation.4 | convolution fusion | flops 1594736640 | bytes 20321280 | tf_op jit(solution)/shard_map/dot_general | solution.py:21
  132.3 75.6 %reduce-scatter.2.cloned.1.call-done = f32[192,2880]{1,0:T(8,128)} async-done(((f32[768,2880]{1,0:T(8,128)}), f32[192,2880]{1,0:T(8,128)}) %reduce-scatter.2.cloned.1.call-update) | async-done | bytes 2211856 | tf_op jit(solution)/shard_map/reduce_scatter | solution.py:68
  207.9 2.8 %convert_element_type.44 = bf16[192,2880]{1,0:T(8,128)(2,1)} convert(f32[192,2880]{1,0:T(8,128)} %reduce-scatter.2.cloned.1.call-done) | non-fusion elementwise | flops 552960 | bytes 3317760 | tf_op jit(solution)/shard_map/convert_element_type | solution.py:74
  210.7 5.5 %all-to-all-start.2 = ((bf16[8,24,2880]{2,1,0:T(8,128)(2,1)}), bf16[8,24,2880]{2,1,0:T(8,128)(2,1)S(1)}, u32[]{:S(2)}, u32[]{:S(2)}) async-start(bf16[8,24,2880]{2,1,0:T(8,128)(2,1)} %bitcast.49), calls=%async_computation.3 | async-start | bytes 2260992 | tf_op jit(solution)/shard_map/all_to_all | solution.py:75
  216.4 5.8 %fusion.1 = bf16[1,2880,360]{1,2,0:T(8,128)(2,1)} fusion(bf16[768,2880]{1,0:T(8,128)(2,1)} %all-gather.5.cloned.1.call-done, bf16[768,360]{0,1:T(8,128)(2,1)} %copy-done.5), kind=kOutput, calls=%fused_computation.9 | convolution fusion | flops 1593561600 | bytes 7050240 | tf_op jit(solution)/shard_map/dot_general | solution.py:15
  222.2 5.7 %fusion = bf16[1,2880,360]{1,2,0:T(8,128)(2,1)} fusion(bf16[768,2880]{1,0:T(8,128)(2,1)} %all-gather.5.cloned.1.call-done, bf16[768,360]{0,1:T(8,128)(2,1)S(1)} %copy-done.7), kind=kOutput, calls=%fused_computation.8 | convolution fusion | flops 1593561600 | bytes 7050240 | tf_op jit(solution)/shard_map/dot_general | solution.py:15
  227.9 3.3 %fusion.2 = bf16[1,360,2880]{2,1,0:T(8,128)(2,1)} fusion(bf16[768,2880]{1,0:T(8,128)(2,1)S(1)} %bitcast.57, f32[768,360]{0,1:T(8,128)S(1)} %copy-done.13, f32[768,360]{0,1:T(8,128)S(1)} %copy-done.12), kind=kOutput, calls=%fused_computation.10 | convolution fusion | flops 1595220480 | bytes 8709120 | tf_op jit(solution)/shard_map/dot_general | solution.py:15
  231.2 12.3 %all-to-all-done.2 = bf16[8,24,2880]{2,1,0:T(8,128)(2,1)S(1)} async-done(((bf16[8,24,2880]{2,1,0:T(8,128)(2,1)}), bf16[8,24,2880]{2,1,0:T(8,128)(2,1)S(1)}, u32[]{:S(2)}, u32[]{:S(2)}) %all-to-all-start.2) | async-done | bytes 1105952 | tf_op jit(solution)/shard_map/all_to_all | solution.py:75
  243.5 1.9 gather_fusion.3
  245.4 1.7 gather.21
  247.1 1.7 reduce_sum.38
  (59 shorter events, 1.8 us)
Async XLA Ops:
  7.2 73.9 %copy-start = (bf16[1,2880,360]{1,2,0:T(8,128)(2,1)S(1)}, bf16[1,2880,360]{1,2,0:T(8,128)(2,1)}, u32[]{:S(2)}) copy-start(bf16[1,2880,360]{1,2,0:T(8,128)(2,1)} %param.11) | copy-start | bytes 6220804
  7.2 1.9 copy-start.1
  7.2 73.9 %all-gather.5.cloned.1.call-start = ((), (), s32[]{:S(2)}) async-start(), calls=%async_computation.5 | async-start | bytes 5652480 | tf_op jit(solution)/shard_map/all_gather | solution.py:52
  10.7 35.5 %copy-start.9 = (f32[32,4]{0,1:T(4,128)S(1)}, f32[32,4]{0,1:T(4,128)}, u32[]{:S(2)}) copy-start(f32[32,4]{0,1:T(4,128)} %param.10) | copy-start | bytes 1540
  10.7 37.3 %copy-start.2 = (bf16[32,2880]{1,0:T(8,128)(2,1)S(1)}, bf16[32,2880]{1,0:T(8,128)(2,1)}, u32[]{:S(2)}) copy-start(bf16[32,2880]{1,0:T(8,128)(2,1)} %param.8) | copy-start | bytes 552964
  46.1 72.9 %all-gather.3.cloned.1.call-start = ((), (), s32[]{:S(2)}) async-start(), calls=%async_computation.4 | async-start | bytes 5652480 | tf_op jit(solution)/shard_map/all_gather | solution.py:53
  80.7 127.2 %reduce-scatter.2.cloned.1.call-start = ((), (), s32[]{:S(2)}) async-start(), calls=%async_computation.6 | async-start | bytes 11304960 | tf_op jit(solution)/shard_map/reduce_scatter | solution.py:68
  81.1 4.3 %copy-start.3 = (bf16[1,2880,360]{1,2,0:T(8,128)(2,1)S(1)}, bf16[1,2880,360]{1,2,0:T(8,128)(2,1)}, u32[]{:S(2)}) copy-start(bf16[1,2880,360]{1,2,0:T(8,128)(2,1)} %param.12) | copy-start | bytes 6220804
  81.1 4.3 %copy-start.10 = (bf16[768,2880]{1,0:T(8,128)(2,1)S(1)}, bf16[768,2880]{1,0:T(8,128)(2,1)}, u32[]{:S(2)}) copy-start(bf16[768,2880]{1,0:T(8,128)(2,1)} %all-gather.5.cloned.1.call-done) | copy-start | bytes 13271044
  85.4 33.5 %copy-start.11 = (f32[768,360]{0,1:T(8,128)}, f32[768,360]{0,1:T(8,128)S(1)}, u32[]{:S(2)}) copy-start(f32[768,360]{0,1:T(8,128)S(1)} %fusion.7) | copy-start | bytes 3317764
  124.3 2.7 %copy-start.6 = (bf16[768,360]{0,1:T(8,128)(2,1)}, bf16[768,360]{0,1:T(8,128)(2,1)S(1)}, u32[]{:S(2)}) copy-start(bf16[768,360]{0,1:T(8,128)(2,1)S(1)} %get-tuple-element.5) | copy-start | bytes 1658884
  124.3 2.7 %copy-start.5 = (bf16[768,360]{0,1:T(8,128)(2,1)}, bf16[768,360]{0,1:T(8,128)(2,1)S(1)}, u32[]{:S(2)}) copy-start(bf16[768,360]{0,1:T(8,128)(2,1)S(1)} %get-tuple-element.4) | copy-start | bytes 1658884
  124.3 2.7 %copy-start.4 = (bf16[1,2880,360]{1,2,0:T(8,128)(2,1)S(1)}, bf16[1,2880,360]{1,2,0:T(8,128)(2,1)}, u32[]{:S(2)}) copy-start(bf16[1,2880,360]{1,2,0:T(8,128)(2,1)} %param.12) | copy-start | bytes 6220804
  132.2 83.9 %copy-start.8 = (s32[32,4]{0,1:T(4,128)S(1)}, s32[32,4]{0,1:T(4,128)}, u32[]{:S(2)}) copy-start(s32[32,4]{0,1:T(4,128)} %param.9) | copy-start | bytes 1540
  210.7 32.9 %all-to-all-start.2 = ((bf16[8,24,2880]{2,1,0:T(8,128)(2,1)}), bf16[8,24,2880]{2,1,0:T(8,128)(2,1)S(1)}, u32[]{:S(2)}, u32[]{:S(2)}) async-start(bf16[8,24,2880]{2,1,0:T(8,128)(2,1)} %bitcast.49), calls=%async_computation.3 | async-start | bytes 2260992 | tf_op jit(solution)/shard_map/all_to_all | solution.py:75
  216.4 5.8 %copy-start.7 = (bf16[768,360]{0,1:T(8,128)(2,1)S(1)}, bf16[768,360]{0,1:T(8,128)(2,1)}, u32[]{:S(2)}) copy-start(bf16[768,360]{0,1:T(8,128)(2,1)} %copy-done.6) | copy-start | bytes 1658884
  216.4 11.5 %slice-start = ((s8[4521984]{0:T(1024)(128)(4,1)}), s8[4194304]{0:T(1024)(128)(4,1)S(1)}, s32[]{:S(2)}) async-start(s8[4521984]{0:T(1024)(128)(4,1)} %bitcast.56), calls=%async_computation.7 | async-start | bytes 8388608
  222.2 5.7 %slice-start.1 = ((s8[4521984]{0:T(1024)(128)(4,1)}), s8[327680]{0:T(1024)(128)(4,1)S(1)}, s32[]{:S(2)}) async-start(s8[4521984]{0:T(1024)(128)(4,1)} %bitcast.56), calls=%async_computation.8 | async-start | bytes 655360
  222.2 5.7 %copy-start.12 = (f32[768,360]{0,1:T(8,128)S(1)}, f32[768,360]{0,1:T(8,128)}, u32[]{:S(2)}) copy-start(f32[768,360]{0,1:T(8,128)} %copy-done.11) | copy-start | bytes 3317764
  222.2 5.7 %copy-start.13 = (f32[768,360]{0,1:T(8,128)S(1)}, f32[768,360]{0,1:T(8,128)}, u32[]{:S(2)}) copy-start(f32[768,360]{0,1:T(8,128)} %fusion.10) | copy-start | bytes 3317764
Sparse Core Ops, SparseCore 0:
  46.2 34.7 all-gather.4
  82.6 36.3 all-gather.2
  132.4 75.4 reduce-scatter.1
where the time goes:
time: 256 us; the launch traced here: 255 us
  waiting for transfers between devices  119 us (46%)
  blocking collectives  66.3 us (26%)
  matrix products  35.2 us (14%)
  between operations  14.1 us (6%)
  local copies, waits for them, and re-layouts  9.49 us (4%)
  other arithmetic  5.75 us (2%)
  starting transfers between devices  5.61 us (2%)
    reduce_scatter x1, waiting for transfers between devices, on_device(): lax.psum_scatter(contract_cols(d_gate, gate_w) + contract_cols(d_upper, u...  75.6 us
    all_to_all x1, blocking collectives, on_device(): lax.all_to_all(send_x, 'expert', split_axis=0, concat_axis=0, tiled=True)  35.4 us
    all_to_all x1, blocking collectives, on_device(): lax.all_to_all(send_dy, 'expert', split_axis=0, concat_axis=0, tiled=True)  30.9 us
    all_gather x1, waiting for transfers between devices, on_device(): lax.all_gather(recv_dy, 'tensor', axis=0, tiled=True)  30.6 us
    dot_general x3, matrix products, contract_rows(): lax.dot_general(left, right, (((0,), (0,)), ((), ())), preferred_element_...  14.7 us
    dot_general x3, matrix products, contract_cols(): lax.dot_general(left, right, (((1,), (1,)), ((), ())), preferred_element_...  13.2 us
    all_to_all x1, waiting for transfers between devices, on_device(): lax.all_to_all(own, 'expert', split_axis=0, concat_axis=0, tiled=True)  12.3 us
    all_to_all x1, starting transfers between devices, on_device(): lax.all_to_all(own, 'expert', split_axis=0, concat_axis=0, tiled=True)  5.49 us
  transfers between devices with their start and end apart: 4, of which 4 were waited for; matrix products, arithmetic and copies ran while one was open for 10% of the time, Pallas kernels for 0%

commit v1 on v0

--- a/solution.py
+++ b/solution.py
@@ -1,7 +1,11 @@
 import jax
 import jax.numpy as jnp
 from jax import lax
+from jax.experimental import pallas as pl
+from jax.experimental.pallas import tpu as pltpu
 from jax.sharding import PartitionSpec as P
+
+MESH = pl.DeviceIdType.MESH
 
 
 def route_slots(flat, experts, cap):
@@ -23,7 +27,7 @@
     )
 
 
-def on_device(tokens, cotangent, routes, combine, w_gate, w_up, w_down):
+def slotted(tokens, cotangent, routes, combine, w_gate, w_up, w_down):
     tok_rows, width = tokens.shape
     top_count = routes.shape[1]
     groups = lax.axis_size("expert")
@@ -80,6 +84,271 @@
     return (token_grad, gate_grad[None], up_grad[None], down_grad[None])
 
 
+def place():
+    e, t = lax.axis_index("expert"), lax.axis_index("tensor")
+    return e // 2, lax.rem(e, 2), t // 2, lax.rem(t, 2)
+
+
+def peers(depth):
+    z, y, x, c = place()
+    e, t = z * 2 + y, x * 2 + c
+    along = [(lax.rem(z + step, depth) * 2 + y, t) for step in range(1, depth)]
+    return along, (z * 2 + 1 - y, t), (e, (1 - x) * 2 + c), (e, x * 2 + 1 - c)
+
+
+def greet(depth):
+    along, over_y, over_x, twin = peers(depth)
+    barrier = pltpu.get_barrier_semaphore()
+    for device in [*along, over_y, over_x, twin]:
+        pl.semaphore_signal(barrier, inc=1, device_id=device, device_id_type=MESH)
+    pl.semaphore_wait(barrier, depth + 2)
+
+
+def gather_kernel(depth, s_in, x_in, d_in, s_out, x_out, d_out, send_sem, recv_sem, local_sem):
+    z, y, x, c = place()
+    along, over_y, over_x, twin = peers(depth)
+    ins, outs = (s_in, x_in, d_in), (s_out, x_out, d_out)
+    sent = [[], [], []]
+
+    def block(dz, dy, dx, dc=0):
+        zz = lax.rem(z + dz, depth)
+        yy, xx, cc = (1 - y if dy else y), (1 - x if dx else x), (1 - c if dc else c)
+        return (zz * 2 + yy) * 4 + xx * 2 + cc
+
+    def send(p, at, device, first=False):
+        copy = pltpu.make_async_remote_copy(
+            src_ref=ins[p] if first else outs[p].at[at],
+            dst_ref=outs[p].at[at],
+            send_sem=send_sem.at[p, len(sent[p])],
+            recv_sem=recv_sem.at[p, at],
+            device_id=device,
+            device_id_type=MESH,
+        )
+        copy.start()
+        sent[p].append(copy)
+
+    def landed(p, at):
+        pltpu.make_async_remote_copy(
+            src_ref=ins[p],
+            dst_ref=outs[p].at[at],
+            send_sem=send_sem.at[p, 0],
+            recv_sem=recv_sem.at[p, at],
+            device_id=twin,
+            device_id_type=MESH,
+        ).wait_recv()
+
+    me = block(0, 0, 0)
+    keep = [pltpu.make_async_copy(ins[p], outs[p].at[me], local_sem.at[p]) for p in range(3)]
+    for copy in keep:
+        copy.start()
+    greet(depth)
+    for device in [over_y, over_x, *along, twin]:
+        for p in range(3):
+            send(p, me, device, True)
+
+    def first_level(dz):
+        at = block(dz, 0, 0)
+        for p in range(3):
+            landed(p, at)
+            for device in (over_x, over_y, twin):
+                send(p, at, device)
+
+    def second_level(dz):
+        by_y, by_x = block(dz, 1, 0), block(dz, 0, 1)
+        for p in range(3):
+            near, far, onward = (by_x, by_y, over_y) if p == 2 else (by_y, by_x, over_x)
+            landed(p, near)
+            send(p, near, onward)
+            send(p, near, twin)
+            landed(p, far)
+            send(p, far, twin)
+
+    for dz in range(1, depth):
+        first_level(dz)
+        second_level(dz - 1)
+    second_level(depth - 1)
+    for dz in range(depth):
+        at = block(dz, 1, 1)
+        for p in range(3):
+            landed(p, at)
+            send(p, at, twin)
+    for dz in range(depth):
+        for dy in range(2):
+            for dx in range(2):
+                for p in range(3):
+                    landed(p, block(dz, dy, dx, 1))
+    for copy in keep:
+        copy.wait()
+    for p in range(3):
+        for copy in sent[p]:
+            copy.wait_send()
+
+
+def gather_all(table, tokens, cotangent):
+    count = lax.axis_size("expert") * lax.axis_size("tensor")
+    depth = lax.axis_size("expert") // 2
+    parts = (table, tokens, cotangent)
+    return pl.pallas_call(
+        lambda *refs: gather_kernel(depth, *refs),
+        out_shape=[jax.ShapeDtypeStruct((count, *a.shape), a.dtype) for a in parts],
+        in_specs=[pl.BlockSpec(memory_space=pltpu.VMEM)] * 3,
+        out_specs=[pl.BlockSpec(memory_space=pl.ANY)] * 3,
+        scratch_shapes=[
+            pltpu.SemaphoreType.DMA((3, count - 1)),
+            pltpu.SemaphoreType.DMA((3, count)),
+            pltpu.SemaphoreType.DMA((3,)),
+        ],
+        compiler_params=pltpu.CompilerParams(collective_id=0, has_side_effects=True),
+    )(*parts)
+
+
+def scatter_kernel(depth, part, out, total, twin_in, x_in, y_in, z_in, send_sem, recv_sem):
+    z, y, x, c = place()
+    along, over_y, over_x, twin = peers(depth)
+    rows = out.shape[0] // 2
+    halves = [pl.ds(0, rows), pl.ds(rows, rows)]
+    sent = []
+
+    def block(dz, dy, dx, dc=0):
+        zz = lax.rem(z + dz, depth)
+        yy, xx, cc = (1 - y if dy else y), (1 - x if dx else x), (1 - c if dc else c)
+        return (zz * 2 + yy) * 4 + xx * 2 + cc
+
+    def send(src, dst, device):
+        copy = pltpu.make_async_remote_copy(
+            src_ref=src,
+            dst_ref=dst,
+            send_sem=send_sem.at[len(sent)],
+            recv_sem=recv_sem.at[len(sent)],
+            device_id=device,
+            device_id_type=MESH,
+        )
+        copy.start()
+        sent.append(copy)
+        return copy
+
+    def add(a, b):
+        return (a.astype(jnp.float32) + b.astype(jnp.float32)).astype(jnp.bfloat16)
+
+    steps = [*range(1, depth), 0]
+    corners = ((1, 1), (0, 1), (1, 0), (0, 0))
+    greet(depth)
+    from_twin, over, last, ends = {}, {}, {}, {}
+    for dz in steps:
+        for dy, dx in corners:
+            i = dz * 4 + dy * 2 + dx
+            from_twin[i] = send(part.at[block(dz, dy, dx, 1)], twin_in.at[i], twin)
+
+    def merge(half, dz, other):
+        over[half, dz, other].wait_recv()
+        if half == 0:
+            i, got = dz * 4 + other * 2, x_in.at[dz * 2 + other]
+        else:
+            i, got = dz * 4 + other, y_in.at[dz * 2 + other]
+        total[i, halves[half]] = add(total[i, halves[half]], got[...])
+        return i
+
+    def first(dz):
+        for dy, dx in corners:
+            i = dz * 4 + dy * 2 + dx
+            from_twin[i].wait_recv()
+            total[i] = add(part[block(dz, dy, dx)], twin_in[i])
+            if dx:
+                over[0, dz, dy] = send(total.at[i, halves[0]], x_in.at[dz * 2 + dy], over_x)
+            if dy:
+                over[1, dz, dx] = send(total.at[i, halves[1]], y_in.at[dz * 2 + dx], over_y)
+
+    def second(dz):
+        i = merge(0, dz, 1)
+        last[0, dz] = send(total.at[i, halves[0]], y_in.at[depth * 2 + dz], over_y)
+        i = merge(1, dz, 1)
+        last[1, dz] = send(total.at[i, halves[1]], x_in.at[depth * 2 + dz], over_x)
+
+    def third(dz):
+        for half in range(2):
+            i = merge(half, dz, 0)
+            last[half, dz].wait_recv()
+            got = (x_in if half else y_in)[depth * 2 + dz]
+            total[i, halves[half]] = add(total[i, halves[half]], got)
+            if dz:
+                ends[half, dz] = send(
+                    total.at[i, halves[half]], z_in.at[half * (depth - 1) + dz - 1], along[dz - 1]
+                )
+
+    for turn in range(depth + 2):
+        for stage, lag in ((first, 0), (second, 1), (third, 2)):
+            if 0 <= turn - lag < depth:
+                stage(steps[turn - lag])
+    for half in range(2):
+        value = total[0, halves[half]].astype(jnp.float32)
+        for dz in range(1, depth):
+            ends[half, dz].wait_recv()
+            value = value + z_in[half * (depth - 1) + dz - 1].astype(jnp.float32)
+        out[halves[half]] = value.astype(jnp.bfloat16)
+    for copy in sent:
+        copy.wait_send()
+
+
+def scatter_sum(part, rows):
+    width = part.shape[1]
+    depth = lax.axis_size("expert") // 2
+    copies = depth * 4 + 2 * (depth * 2 + depth + depth - 1)
+    half = rows // 2
+    return pl.pallas_call(
+        lambda *refs: scatter_kernel(depth, *refs),
+        out_shape=jax.ShapeDtypeStruct((rows, width), jnp.bfloat16),
+        in_specs=[pl.BlockSpec(memory_space=pltpu.VMEM)],
+        out_specs=pl.BlockSpec(memory_space=pltpu.VMEM),
+        scratch_shapes=[
+            pltpu.VMEM((depth * 4, rows, width), jnp.bfloat16),
+            pltpu.VMEM((depth * 4, rows, width), jnp.bfloat16),
+            pltpu.VMEM((depth * 3, half, width), jnp.bfloat16),
+            pltpu.VMEM((depth * 3, half, width), jnp.bfloat16),
+            pltpu.VMEM((depth * 2 - 2, half, width), jnp.bfloat16),
+            pltpu.SemaphoreType.DMA((copies,)),
+            pltpu.SemaphoreType.DMA((copies,)),
+        ],
+        compiler_params=pltpu.CompilerParams(
+            collective_id=1, has_side_effects=True, vmem_limit_bytes=48 * 1024 * 1024
+        ),
+    )(part.reshape(-1, rows, width))
+
+
+def dense(tokens, cotangent, routes, combine, w_gate, w_up, w_down):
+    rows, width = tokens.shape
+    experts = lax.axis_size("expert") * w_gate.shape[0]
+    named = routes[:, :, None] == jnp.arange(experts, dtype=jnp.int32)[None, None, :]
+    table = jnp.sum(jnp.where(named, combine[:, :, None], 0.0), axis=1).T
+    table, xs, cot = gather_all(table, tokens, cotangent)
+    xs = xs.reshape(-1, width)
+    scale = lax.dynamic_slice_in_dim(table, lax.axis_index("expert"), 1, axis=1).reshape(-1, 1)
+    dys = (scale * cot.reshape(-1, width).astype(jnp.float32)).astype(jnp.bfloat16)
+    gate_w = w_gate[0]
+    up_w = w_up[0]
+    down_w = w_down[0]
+    gate = jnp.dot(xs, gate_w, preferred_element_type=jnp.float32)
+    upper = jnp.dot(xs, up_w, preferred_element_type=jnp.float32)
+    sigma = jax.nn.sigmoid(gate)
+    act = (gate * sigma * upper).astype(jnp.bfloat16)
+    d_act = contract_cols(dys, down_w)
+    d_upper = (d_act * gate * sigma).astype(jnp.bfloat16)
+    d_gate = (d_act * upper * sigma * (1.0 + gate * (1.0 - sigma))).astype(jnp.bfloat16)
+    part = contract_cols(d_gate, gate_w) + contract_cols(d_upper, up_w)
+    token_grad = scatter_sum(part.astype(jnp.bfloat16), rows)
+    down_grad = contract_rows(act, dys).astype(jnp.bfloat16)
+    gate_grad = contract_rows(xs, d_gate).astype(jnp.bfloat16)
+    up_grad = contract_rows(xs, d_upper).astype(jnp.bfloat16)
+    return (token_grad, gate_grad[None], up_grad[None], down_grad[None])
+
+
+def on_device(tokens, cotangent, routes, combine, w_gate, w_up, w_down):
+    groups, shards = lax.axis_size("expert"), lax.axis_size("tensor")
+    rows, top_count = routes.shape
+    few = w_gate.shape[0] == 1 and groups <= 2 * top_count
+    plan = dense if few and shards == 4 and groups % 2 == 0 and rows % 32 == 0 else slotted
+    return plan(tokens, cotangent, routes, combine, w_gate, w_up, w_down)
+
+
 def solution(mesh):
     in_specs = (
         P(("expert", "tensor"), None),

time: 256 us -> 181 us (0.71)
  waiting for transfers between devices: 119 us -> 0 us
  Pallas kernels: 0 us -> 118 us
  blocking collectives: 66.3 us -> 0 us
  between operations: 14.1 us -> 0.72 us
  starting transfers between devices: 5.61 us -> 0 us
  local copies, waits for them, and re-layouts: 9.49 us -> 14.1 us
  matrix products: 35.2 us -> 39.8 us
    pallas_call x0 -> x2, Pallas kernels: none -> 118 us  [the longest x1 68.4 us: gather_all(): pl.pallas_call(lambda *refs: gather_kernel(depth, *refs), out_shape=[jax....]
    reduce_scatter x1 -> x0, waiting for transfers between devices: 75.6 us -> none  [on_device(): lax.psum_scatter(contract_cols(d_gate, gate_w) + contract_cols(d_upper, u...]
    all_to_all x2 -> x0, blocking collectives: 66.3 us -> none  [the longest x1 35.4 us: on_device(): lax.all_to_all(send_x, 'expert', split_axis=0, concat_axis=0, tiled=True)]
    all_gather x2 -> x0, waiting for transfers between devices: 30.9 us -> none  [the longest x1 30.6 us: on_device(): lax.all_gather(recv_dy, 'tensor', axis=0, tiled=True)]
    all_to_all x1 -> x0, waiting for transfers between devices: 12.3 us -> none  [on_device(): lax.all_to_all(own, 'expert', split_axis=0, concat_axis=0, tiled=True)]
    convert_element_type x0 -> x1, local copies, waits for them, and re-layouts: none -> 8.52 us  [dense(): token_grad = scatter_sum(part.astype(jnp.bfloat16), rows)]
    gather x5 -> x0, local copies, waits for them, and re-layouts: 7.81 us -> none  [the longest x2 3.56 us: on_device(): picked = back[slot].astype(jnp.float32).reshape(tok_rows, top_count, width)]
    all_to_all x1 -> x0, starting transfers between devices: 5.49 us -> none  [on_device(): lax.all_to_all(own, 'expert', split_axis=0, concat_axis=0, tiled=True)]
  transfers between devices with their start and end apart: 4 -> 0, of which waited for: 4 -> 0; matrix products, arithmetic and copies ran while one was open for 10% -> 0% of each run, Pallas kernels for 0% -> 0%
where the time goes in v1:
time: 181 us
  Pallas kernels  118 us (65%)
  matrix products  39.8 us (22%)
  local copies, waits for them, and re-layouts  14.1 us (8%)
  other arithmetic  8.02 us (4%)
    pallas_call x1, Pallas kernels, gather_all(): pl.pallas_call(lambda *refs: gather_kernel(depth, *refs), out_shape=[jax....  68.4 us
    pallas_call x1, Pallas kernels, scatter_sum(): pl.pallas_call(lambda *refs: scatter_kernel(depth, *refs), out_shape=jax....  49.6 us
    dot_general x3, matrix products, contract_rows(): lax.dot_general(left, right, (((0,), (0,)), ((), ())), preferred_element_...  17.9 us
    dot_general x3, matrix products, contract_cols(): lax.dot_general(left, right, (((1,), (1,)), ((), ())), preferred_element_...  11.7 us
    convert_element_type x1, local copies, waits for them, and re-layouts, dense(): token_grad = scatter_sum(part.astype(jnp.bfloat16), rows)  8.52 us
    convert_element_type x2, other arithmetic, dense(): (scale * cot.reshape(-1, width).astype(jnp.float32)).astype(jnp.bfloat16)  6.57 us
    dot_general x1, matrix products, dense(): gate = jnp.dot(xs, gate_w, preferred_element_type=jnp.float32)  6.46 us
    dot_general x1, matrix products, dense(): upper = jnp.dot(xs, up_w, preferred_element_type=jnp.float32)  3.64 us

profile of v1, /device:TPU:0, one launch (start us, length us, event | category | flops | bytes accessed | tf_op | source)
XLA Modules:
  0.0 180.7 jit_solution(2472327034074490728)
XLA Ops:
  0.6 0.0 copy-start
  0.7 1.4 select_reduce_fusion
  2.1 68.4 %shard_map.102 = (f32[32,8,32]{2,1,0:T(8,128)}, bf16[32,32,2880]{2,1,0:T(8,128)(2,1)}, bf16[32,32,2880]{2,1,0:T(8,128)(2,1)}) custom-call(f32[8,32]{1,0:T(8,128)} %bitcast.45, bf16[32,2880]{1,0:T(8,128)(2,1)} %refs_1_.1, bf16[32,2880]{1,0:T(8,128)(2,1)} %refs_2_.1), custom_call_target="tpu_custom_call" | custom-call | tf_op jit(solution)/shard_map/pallas_call | solution.py:191
  70.5 0.5 broadcast.17
  71.0 1.6 fusion.15
  72.6 0.1 mul.52
  72.7 6.5 %fusion.6 = f32[1024,360]{0,1:T(8,128)} fusion(bf16[1024,2880]{1,0:T(8,128)(2,1)} %bitcast.46, bf16[1,2880,360]{1,2,0:T(8,128)(2,1)S(1)} %copy-done), kind=kOutput, calls=%fused_computation.12 | convolution fusion | flops 2123366400 | bytes 9446400 | tf_op jit(solution)/shard_map/dot_general | solution.py:329
  79.2 0.0 copy-done.3
  79.2 3.6 %fusion.9 = f32[1024,360]{0,1:T(8,128)} fusion(bf16[1024,2880]{1,0:T(8,128)(2,1)S(1)} %bitcast.48, bf16[1,2880,360]{1,2,0:T(8,128)(2,1)S(1)} %copy-done.2), kind=kOutput, calls=%fused_computation.15 | convolution fusion | flops 2123366400 | bytes 9446400 | tf_op jit(solution)/shard_map/dot_general | solution.py:330
  82.8 0.0 slice-done
  82.8 2.0 %multiply_convert_fusion = bf16[32,32,2880]{2,1,0:T(8,128)(2,1)S(1)} fusion(f32[32,32]{1,0:T(8,128)S(1)} %bitcast.44, bf16[32,32,2880]{2,1,0:T(8,128)(2,1)S(1)} %bitcast.42), kind=kLoop, calls=%fused_computation.2 | loop fusion | flops 8847360 | bytes 11800576 | tf_op jit(solution)/shard_map/convert_element_type | solution.py:325
  84.8 4.6 %fusion = bf16[1024,2880]{1,0:T(8,128)(2,1)} fusion(f32[1024]{0:T(1024)S(1)} %mul.52, bf16[32,32,2880]{2,1,0:T(8,128)(2,1)S(1)} %bitcast.42), kind=kLoop, calls=%fused_computation.1 | loop fusion | flops 8847360 | bytes 11800576 | tf_op jit(solution)/shard_map/convert_element_type | solution.py:325
  89.4 7.6 %fusion.3 = bf16[1,360,2880]{2,1,0:T(8,128)(2,1)} fusion(bf16[1024,2880]{1,0:T(8,128)(2,1)} %fusion, f32[1024,360]{0,1:T(8,128)} %fusion.9, f32[1024,360]{0,1:T(8,128)} %fusion.6), kind=kOutput, calls=%fused_computation.9 | convolution fusion | flops 2126615040 | bytes 10920960 | tf_op jit(solution)/shard_map/dot_general | solution.py:19
  97.0 0.0 copy-done.4
  97.0 0.0 slice-start.3
  97.0 3.1 %multiply_convert_fusion.2 = (bf16[1024,360]{0,1:T(8,128)(2,1)S(1)}, bf16[1024,360]{0,1:T(8,128)(2,1)S(1)}) fusion(f32[1024,360]{0,1:T(8,128)S(1)} %copy-done.5, f32[1024,360]{0,1:T(8,128)S(1)} %copy-done.6, bf16[1024,2880]{1,0:T(8,128)(2,1)S(1)} %bitcast.43, bf16[1,360,2880]{2,1,0:T(8,128)(2,1)S(1)} %copy-done.4), kind=kOutput, calls=%fused_computation.20 | convolution fusion | flops 2128158720 | bytes 12395520 | tf_op jit(solution)/shard_map/dot_general | solution.py:25
  100.1 6.5 %fusion.2 = bf16[1,2880,360]{1,2,0:T(8,128)(2,1)} fusion(bf16[1024,2880]{1,0:T(8,128)(2,1)} %bitcast.47, bf16[1024,360]{0,1:T(8,128)(2,1)S(1)} %get-tuple-element.12), kind=kOutput, calls=%fused_computation.8 | convolution fusion | flops 2124403200 | bytes 8709120 | tf_op jit(solution)/shard_map/dot_general | solution.py:19
  106.6 3.9 %fusion.1 = bf16[1,2880,360]{1,2,0:T(8,128)(2,1)} fusion(bf16[1024,2880]{1,0:T(8,128)(2,1)S(1)} %bitcast.51, bf16[1024,360]{0,1:T(8,128)(2,1)S(1)} %get-tuple-element.13), kind=kOutput, calls=%fused_computation.7 | convolution fusion | flops 2124403200 | bytes 8709120 | tf_op jit(solution)/shard_map/dot_general | solution.py:19
  110.4 3.3 %fusion.4 = f32[1024,2880]{0,1:T(8,128)S(1)} fusion(bf16[1024,360]{0,1:T(8,128)(2,1)S(1)} %get-tuple-element.13, bf16[1,2880,360]{1,2,0:T(8,128)(2,1)S(1)} %copy-done), kind=kOutput, calls=%fused_computation.10 | convolution fusion | flops 2123366400 | bytes 14607360 | tf_op jit(solution)/shard_map/dot_general | solution.py:25
  113.8 5.3 %add_convert_fusion = bf16[1024,2880]{0,1:T(8,128)(2,1)} fusion(f32[1024,2880]{0,1:T(8,128)S(1)} %fusion.4, bf16[1024,360]{0,1:T(8,128)(2,1)S(1)} %get-tuple-element.12, bf16[1,2880,360]{1,2,0:T(8,128)(2,1)S(1)} %copy-done.2), kind=kOutput, calls=%fused_computation.3 | convolution fusion | flops 2129264640 | bytes 20505600 | tf_op jit(solution)/shard_map/dot_general | solution.py:25
  119.1 8.5 %copy.14 = bf16[1024,2880]{1,0:T(8,128)(2,1)} copy(bf16[1024,2880]{0,1:T(8,128)(2,1)} %add_convert_fusion) | data formatting | bytes 11796480 | tf_op jit(solution)/shard_map/convert_element_type | solution.py:337
  127.6 2.7 %copy-done.1 = bf16[1024,2880]{1,0:T(8,128)(2,1)S(1)} copy-done((bf16[1024,2880]{1,0:T(8,128)(2,1)S(1)}, bf16[1024,2880]{1,0:T(8,128)(2,1)}, u32[]{:S(2)}) %copy-start.1) | copy-done | bytes 5898264
  130.3 49.6 %shard_map.103 = bf16[32,2880]{1,0:T(8,128)(2,1)S(1)} custom-call(bf16[32,32,2880]{2,1,0:T(8,128)(2,1)S(1)} %bitcast.40), custom_call_target="tpu_custom_call" | custom-call | tf_op jit(solution)/shard_map/pallas_call | solution.py:297
  180.0 0.7 copy.16
  (18 shorter events, 0.0 us)
Async XLA Ops:
  0.6 72.1 %copy-start = (bf16[1,2880,360]{1,2,0:T(8,128)(2,1)S(1)}, bf16[1,2880,360]{1,2,0:T(8,128)(2,1)}, u32[]{:S(2)}) copy-start(bf16[1,2880,360]{1,2,0:T(8,128)(2,1)} %param.11) | copy-start | bytes 6220804
  72.7 6.5 %copy-start.2 = (bf16[1,2880,360]{1,2,0:T(8,128)(2,1)S(1)}, bf16[1,2880,360]{1,2,0:T(8,128)(2,1)}, u32[]{:S(2)}) copy-start(bf16[1,2880,360]{1,2,0:T(8,128)(2,1)} %param.12) | copy-start | bytes 6220804
  72.7 6.5 %copy-start.3 = (bf16[32,32,2880]{2,1,0:T(8,128)(2,1)S(1)}, bf16[32,32,2880]{2,1,0:T(8,128)(2,1)}, u32[]{:S(2)}) copy-start(bf16[32,32,2880]{2,1,0:T(8,128)(2,1)} %get-tuple-element.9) | copy-start | bytes 17694724
  72.7 10.1 %slice-start = ((s8[6029312]{0:T(1024)(128)(4,1)}), s8[4194304]{0:T(1024)(128)(4,1)S(1)}, s32[]{:S(2)}) async-start(s8[6029312]{0:T(1024)(128)(4,1)} %bitcast.41), calls=%async_computation | async-start | bytes 8388608
  79.2 3.6 %slice-start.1 = ((s8[6029312]{0:T(1024)(128)(4,1)}), s8[1835008]{0:T(1024)(128)(4,1)S(1)}, s32[]{:S(2)}) async-start(s8[6029312]{0:T(1024)(128)(4,1)} %bitcast.41), calls=%async_computation.1 | async-start | bytes 3670016
  89.4 7.6 %copy-start.4 = (bf16[1,360,2880]{2,1,0:T(8,128)(2,1)S(1)}, bf16[1,360,2880]{2,1,0:T(8,128)(2,1)}, u32[]{:S(2)}) copy-start(bf16[1,360,2880]{2,1,0:T(8,128)(2,1)} %param.13) | copy-start | bytes 6220804
  89.4 7.6 %copy-start.5 = (f32[1024,360]{0,1:T(8,128)S(1)}, f32[1024,360]{0,1:T(8,128)}, u32[]{:S(2)}) copy-start(f32[1024,360]{0,1:T(8,128)} %fusion.6) | copy-start | bytes 4423684
  89.4 7.6 %copy-start.6 = (f32[1024,360]{0,1:T(8,128)S(1)}, f32[1024,360]{0,1:T(8,128)}, u32[]{:S(2)}) copy-start(f32[1024,360]{0,1:T(8,128)} %fusion.9) | copy-start | bytes 4423684
  89.4 17.2 %slice-start.2 = ((s8[6029312]{0:T(1024)(128)(4,1)}), s8[4194304]{0:T(1024)(128)(4,1)S(1)}, s32[]{:S(2)}) async-start(s8[6029312]{0:T(1024)(128)(4,1)} %bitcast.49), calls=%async_computation.2 | async-start | bytes 8388608
  97.0 9.6 %slice-start.3 = ((s8[6029312]{0:T(1024)(128)(4,1)}), s8[1835008]{0:T(1024)(128)(4,1)S(1)}, s32[]{:S(2)}) async-start(s8[6029312]{0:T(1024)(128)(4,1)} %bitcast.49), calls=%async_computation.3 | async-start | bytes 3670016
  127.6 2.7 %copy-start.1 = (bf16[1024,2880]{1,0:T(8,128)(2,1)S(1)}, bf16[1024,2880]{1,0:T(8,128)(2,1)}, u32[]{:S(2)}) copy-start(bf16[1024,2880]{1,0:T(8,128)(2,1)} %copy.14) | copy-start | bytes 17694724
